TPU v7x, 32 devices: a whole 2x2x4 slice. The times are simulated.
32 devices in a mesh: gx: 4 (over y, x), gy: 2 (over core), gz: 4 (over z).
Axes of the slice: x: 2, y: 2, z: 4, core: 2. Of those that a mesh axis runs over, the one named last changes fastest.
Arguments:
- measures: float32 [65536, 256], P(('gx', 'gy', 'gz')), may hold values from -6 to 6
- group_index: int32 [65536], P(('gx', 'gy', 'gz')), may hold values from 0 to 511, as said below
- distinct_keys: int32 [32, 512], P(('gx', 'gy', 'gz')), may hold values from 32 to 65567, as said below
- group_counts: int32 [32], P(('gx', 'gy', 'gz')), may hold values from 128 to 512, as said below
Outputs:
- group_sums: float32 [16384, 256], P(('gx', 'gy', 'gz'))
- group_rows: int32 [16384], P(('gx', 'gy', 'gz'))
- group_keys: int32 [16384], P(('gx', 'gy', 'gz'))
- group_total: int32 [], replicated
Inputs may be any that keep to these rules, and one draw needn't show every extreme that they name: `group_counts`: every device has between 128 and 512 groups, and some device has exactly 512. `group_index`: each row's index lies below its device's group count, and every group of a device has at least one row. `distinct_keys`: each device's keys rise strictly; all keys of device d equal d modulo 32, so no key lives on two devices; entries at and past the device's count are unused.
All inputs are finite; a program needn't handle non-finite values.
Results may differ from a plain program's by a relative error of at most 0.0003.
Values sent between devices are 32-bit elements; how exact they have to be, the bound alone decides.
A program may use at most 64 MiB of HBM per device.

v0:
```python
import functools

import jax
import jax.numpy as jnp
from jax import lax
from jax.experimental import pallas as pl
from jax.experimental.pallas import tpu as pltpu
from jax.sharding import PartitionSpec as P

AXES = ("gx", "gy", "gz")
LANES = 128
MESH = pl.DeviceIdType.MESH


def round_up(value, unit):
    return (value + unit - 1) // unit * unit


def steps_of(dims):
    nx, ny, nz = dims
    far = [(a, b, c) for c in range(nz) for a in range(nx) for b in range(ny)]
    far.sort(key=lambda k: -min(k[2], nz - k[2]))
    return [((a * ny + b) * nz + c, (a, b, c)) for a, b, c in far if (a, b, c) != (0, 0, 0)]


def wrapped(value, size):
    return jnp.where(value >= size, value - size, value)


def modulo(value, size):
    if size & (size - 1) == 0:
        return value & (size - 1)
    return lax.rem(value, size)


def divide(value, size):
    if size & (size - 1) == 0:
        return lax.shift_right_arithmetic(value, jnp.int32(size.bit_length() - 1))
    return value // size


def exchange_kernel(
    shape,
    index_hbm,
    keys_hbm,
    count_hbm,
    measures_ref,
    recv_ref,
    counts_ref,
    held,
    stage,
    send,
    tally_ref,
    cbuf,
    index_ref,
    keys_ref,
    count_ref,
    small_sem,
    load_sem,
    count_sem,
    data_sem,
):
    dims, span, levels, chunks, fields_at = shape
    nx, ny, nz = dims
    devices = nx * ny * nz
    spots = [lax.axis_index(axis) for axis in AXES]
    me = (spots[0] * ny + spots[1]) * nz + spots[2]
    ring = [[wrapped(spot + k, size) for k in range(size)] for spot, size in zip(spots, dims)]
    rows, width = held.shape
    chunk = rows // chunks
    halves = width // LANES
    sent_rows = fields_at + 2
    steps = steps_of(dims)

    count_load = pltpu.make_async_copy(count_hbm, count_ref, small_sem.at[0])
    count_load.start()
    barrier = pltpu.get_barrier_semaphore()
    for _, k in steps:
        pl.semaphore_signal(
            barrier, inc=1, device_id=tuple(r[i] for r, i in zip(ring, k)), device_id_type=MESH
        )
    index_load = pltpu.make_async_copy(index_hbm, index_ref, small_sem.at[1])
    index_load.start()
    loads = []
    for c in range(chunks):
        piece = pl.ds(c * chunk, chunk)
        load = pltpu.make_async_copy(measures_ref.at[piece], held.at[piece], load_sem.at[c])
        load.start()
        loads.append(load)
    keys_load = pltpu.make_async_copy(keys_hbm, keys_ref, small_sem.at[2])
    keys_load.start()

    def remote(source, goal, sems, k):
        return pltpu.make_async_remote_copy(
            src_ref=source,
            dst_ref=goal,
            send_sem=sems.at[0],
            recv_sem=sems.at[1],
            device_id=tuple(r[i] for r, i in zip(ring, k)),
            device_id_type=MESH,
        )

    count_load.wait()
    cbuf[0] = jnp.broadcast_to(count_ref[...], cbuf.shape[1:])
    index_load.wait()

    row = lax.broadcasted_iota(jnp.int32, (span, LANES), 0)
    labels = lax.rem(row, levels) * devices + row // levels

    total = None
    for c in range(chunks):
        loads[c].wait()
        x = held[pl.ds(c * chunk, chunk), :]
        high = x.astype(jnp.bfloat16)
        low = (x - high.astype(jnp.float32)).astype(jnp.bfloat16)
        parts = []
        for j in range(chunk // LANES):
            at = c * (chunk // LANES) + j
            hit = jnp.where(index_ref[pl.ds(at, 1), :] == labels, 1.0, 0.0)
            if at == 0:
                tally_ref[...] = hit
            else:
                tally_ref[...] += hit
            parts.append(hit.astype(jnp.bfloat16))
        hits = jnp.concatenate(parts, axis=1)
        dot = functools.partial(jnp.dot, preferred_element_type=jnp.float32)
        part = dot(hits, high) + dot(hits, low)
        for h in range(halves):
            block = part[:, h * LANES : (h + 1) * LANES].reshape(devices, levels, LANES)
            if c == 0:
                stage[:, h * levels : (h + 1) * levels, :] = block
            else:
                stage[:, h * levels : (h + 1) * levels, :] += block
        if c == 0:
            pl.semaphore_wait(barrier, devices - 1)
            for slot, k in steps:
                remote(cbuf.at[0], cbuf.at[slot], count_sem, k).start()

    tallies = lax.dot_general(
        jnp.ones((8, LANES), jnp.bfloat16),
        tally_ref[...].astype(jnp.bfloat16),
        (((1,), (1,)), ((), ())),
        preferred_element_type=jnp.float32,
    )[0:1]
    keys_load.wait()
    keys = keys_ref[...]
    source = lax.broadcasted_iota(jnp.int32, (span, span), 0)
    goal = lax.broadcasted_iota(jnp.int32, (span, span), 1)
    moved = (source == lax.rem(goal, levels) * devices + goal // levels)
    moved = jnp.where(moved, 1.0, 0.0).astype(jnp.bfloat16)
    line = lax.broadcasted_iota(jnp.int32, (8, span), 0)
    pieces = jnp.where(
        line == 0, keys & 255, jnp.where(line == 1, (keys >> 8) & 255, (keys >> 16) & 255)
    )
    pieces = jnp.dot(
        pieces.astype(jnp.float32).astype(jnp.bfloat16), moved, preferred_element_type=jnp.float32
    )
    placed = pieces[0:1] + pieces[1:2] * 256.0 + pieces[2:3] * 65536.0
    fields = jnp.concatenate([tallies, placed], axis=0)
    for a in range(devices):
        tile = a * levels // LANES * LANES
        stage[a, fields_at : fields_at + 2, :] = fields[:, tile : tile + LANES]

    others = cbuf.at[pl.ds(1, devices - 1)]
    pltpu.make_async_copy(others, others, count_sem.at[1]).wait()
    counts = cbuf[...][:, 0, :]
    slots = lax.broadcasted_iota(jnp.int32, counts.shape, 0)
    parts = (divide(slots, ny * nz), modulo(divide(slots, nz), ny), modulo(slots, nz))
    back = [
        jnp.where(spot >= part, spot - part, spot - part + size)
        for spot, part, size in zip(spots, parts, dims)
    ]
    sender = (back[0] * ny + back[1]) * nz + back[2]
    lane = lax.broadcasted_iota(jnp.int32, counts.shape, 1)
    counts_ref[...] = jnp.sum(jnp.where(sender == lane, counts, 0), axis=0, keepdims=True)
    before = jnp.sum(jnp.where(sender < me, counts, 0), axis=0, keepdims=True)[0, 0]
    shift = modulo(before, devices)

    for slot, (a, b, c) in steps:
        other = (ring[0][a] * ny + ring[1][b]) * nz + ring[2][c]
        send[slot] = stage[modulo(other - shift + devices, devices)]
    for slot, k in steps:
        piece = pl.ds(0, sent_rows)
        remote(send.at[slot, piece], recv_ref.at[slot, piece], data_sem, k).start()
    recv_ref[0] = stage[modulo(me - shift + devices, devices)]
    pltpu.make_async_copy(others, others, count_sem.at[0]).wait()
    landed = recv_ref.at[pl.ds(1, devices - 1), pl.ds(0, sent_rows)]
    left = send.at[pl.ds(1, devices - 1), pl.ds(0, sent_rows)]
    pltpu.make_async_copy(left, left, data_sem.at[0]).wait()
    pltpu.make_async_copy(landed, landed, data_sem.at[1]).wait()


def place_kernel(
    shape, counts_ref, recv_ref, sums_ref, rows_ref, keys_ref, total_ref, buf
):
    dims, span, levels, fields_at = shape
    nx, ny, nz = dims
    devices = nx * ny * nz
    spots = [lax.axis_index(axis) for axis in AXES]
    me = (spots[0] * ny + spots[1]) * nz + spots[2]
    back = [
        [jnp.where(spot >= k, spot - k, spot - k + size) for k in range(size)]
        for spot, size in zip(spots, dims)
    ]
    halves = sums_ref.shape[1] // LANES
    lane = lax.broadcasted_iota(jnp.int32, (8, span), 1)
    fields = jnp.zeros((8, span), jnp.float32)
    offset = jnp.int32(0)

    for d in range(devices):
        slot = (back[0][d // (ny * nz)] * ny + back[1][d // nz % ny]) * nz + back[2][d % nz]
        first = modulo(me - modulo(offset, devices) + devices, devices)
        start = divide(offset + first, devices)
        for h in range(halves):
            buf[h, pl.ds(start, levels), :] = recv_ref[slot, h * levels : (h + 1) * levels, :]
        turn = modulo(modulo(start, LANES) - modulo(first * levels, LANES) + LANES, LANES)
        turned = pltpu.roll(recv_ref[slot, fields_at : fields_at + 8, :], turn, 1)
        wide = jnp.concatenate([turned] * (span // LANES), axis=1)
        fields = jnp.where(lane >= start, wide, fields)
        offset = offset + counts_ref[0, d]

    total_ref[0, 0] = offset
    taken = divide(offset - me + devices - 1, devices)
    row = lax.broadcasted_iota(jnp.int32, (span, LANES), 0)
    for h in range(halves):
        sums_ref[:, h * LANES : (h + 1) * LANES] = jnp.where(row < taken, buf[h, 0:span, :], 0.0)
    inside = lane[0:1] < taken
    rows_ref[...] = jnp.where(inside, fields[0:1].astype(jnp.int32), 0)
    keys_ref[...] = jnp.where(inside, fields[1:2].astype(jnp.int32), -1)


def shards(measures, group_index, distinct_keys, group_counts):
    rows, width = measures.shape
    span = distinct_keys.shape[1]
    dims = tuple(lax.axis_size(axis) for axis in AXES)
    devices = dims[0] * dims[1] * dims[2]
    levels = span // devices
    chunks = 4 if rows % (4 * LANES) == 0 else 1
    fields_at = round_up(levels * (width // LANES), 8)
    slab = fields_at + 8
    wide = round_up(devices, LANES)
    vmem = pl.BlockSpec(memory_space=pltpu.VMEM)
    smem = pl.BlockSpec(memory_space=pltpu.SMEM)
    anywhere = pl.BlockSpec(memory_space=pl.ANY)
    received, counts = pl.pallas_call(
        functools.partial(
            exchange_kernel, (dims, span, levels, chunks, fields_at)
        ),
        out_shape=(
            pltpu.VMEM((devices, slab, LANES), jnp.float32),
            pltpu.VMEM((1, wide), jnp.int32),
        ),
        in_specs=[anywhere] * 4,
        out_specs=(vmem, vmem),
        scratch_shapes=[
            pltpu.VMEM((rows, width), jnp.float32),
            pltpu.VMEM((devices, slab, LANES), jnp.float32),
            pltpu.VMEM((devices, slab, LANES), jnp.float32),
            pltpu.VMEM((span, LANES), jnp.float32),
            pltpu.VMEM((devices, 1, wide), jnp.int32),
            pltpu.VMEM((rows // LANES, LANES), jnp.int32),
            pltpu.VMEM((1, span), jnp.int32),
            pltpu.VMEM((1, 1), jnp.int32),
            pltpu.SemaphoreType.DMA((3,)),
            pltpu.SemaphoreType.DMA((chunks,)),
            pltpu.SemaphoreType.DMA((2,)),
            pltpu.SemaphoreType.DMA((2,)),
        ],
        compiler_params=pltpu.CompilerParams(collective_id=0, has_side_effects=True),
        name="exchange",
    )(group_index.reshape(rows // LANES, LANES), distinct_keys, group_counts.reshape(1, 1), measures)
    sums, tallies, keys, total = pl.pallas_call(
        functools.partial(place_kernel, (dims, span, levels, fields_at)),
        out_shape=(
            jax.ShapeDtypeStruct((span, width), jnp.float32),
            jax.ShapeDtypeStruct((1, span), jnp.int32),
            jax.ShapeDtypeStruct((1, span), jnp.int32),
            jax.ShapeDtypeStruct((1, 1), jnp.int32),
        ),
        in_specs=[smem, vmem],
        out_specs=(vmem, vmem, vmem, smem),
        scratch_shapes=[pltpu.VMEM((width // LANES, span + round_up(levels, 8), LANES), jnp.float32)],
        compiler_params=pltpu.CompilerParams(vmem_limit_bytes=16 * 1024 * 1024),
        name="place",
    )(*(pltpu.with_memory_space_constraint(part, pltpu.VMEM) for part in (counts, received)))
    return sums, tallies.reshape(span), keys.reshape(span), total.reshape(())


def solution(mesh):
    return jax.shard_map(
        shards,
        mesh=mesh,
        in_specs=(
            P(AXES, None),
            P(AXES),
            P(AXES, None),
            P(AXES),
        ),
        out_specs=(P(AXES, None), P(AXES), P(AXES), P()),
        check_vma=False,
    )
```

profile of v0, /device:TPU:13, one launch (start us, length us, event | category | flops | bytes accessed | tf_op | source)
XLA Modules:
  0.0 25.8 jit_solution(12453018492436540009)
XLA Ops:
  1.3 22.9 %exchange.1 = (f32[32,40,128]{2,1,0:T(8,128)S(1)}, s32[1,128]{1,0:T(1,128)S(1)}) custom-call(s32[16,128]{1,0:T(8,128)} %bitcast.6, s32[1,512]{1,0:T(1,128)} %keys_hbm.1, s32[1,1]{1,0:T(1,128)} %bitcast.5.count_hbm, f32[2048,256]{1,0:T(8,128)} %measures_ref.1), custom_call_target="tpu_custom_call" | custom-call | tf_op jit(solution)/shard_map/exchange/pallas_call | solution.py:245
  24.2 1.6 %place.1 = (f32[512,256]{1,0:T(8,128)}, s32[1,512]{1,0:T(1,128)}, s32[1,512]{1,0:T(1,128)}, s32[1,1]{1,0:T(1,128)}) custom-call(s32[1,128]{1,0:T(1,128)S(1)} %get-tuple-element.10.counts_ref, f32[32,40,128]{2,1,0:T(8,128)S(1)} %get-tuple-element.11.recv_ref), custom_call_target="tpu_custom_call" | custom-call | tf_op jit(solution)/shard_map/place/pallas_call | solution.py:272
where the time goes:
time: 26.1 us; the launch traced here: 25.8 us
  Pallas kernels  24.5 us (94%)
  between operations  1.29 us (5%)
    pallas_call x1, Pallas kernels, shards(): pl.pallas_call(functools.partial(exchange_kernel, (dims, span, levels, ch...  22.9 us
    pallas_call x1, Pallas kernels, shards(): pl.pallas_call(functools.partial(place_kernel, (dims, span, levels, field...  1.63 us

commit v1 on v0

--- a/solution.py
+++ b/solution.py
@@ -16,11 +16,10 @@
     return (value + unit - 1) // unit * unit
 
 
-def steps_of(dims):
+def relative_steps(dims):
     nx, ny, nz = dims
-    far = [(a, b, c) for c in range(nz) for a in range(nx) for b in range(ny)]
-    far.sort(key=lambda k: -min(k[2], nz - k[2]))
-    return [((a * ny + b) * nz + c, (a, b, c)) for a, b, c in far if (a, b, c) != (0, 0, 0)]
+    steps = [(a, b, c) for c in range(nz) for a in range(nx) for b in range(ny)]
+    return [k for k in steps if k != (0, 0, 0)]
 
 
 def wrapped(value, size):
@@ -37,6 +36,26 @@
     if size & (size - 1) == 0:
         return lax.shift_right_arithmetic(value, jnp.int32(size.bit_length() - 1))
     return value // size
+
+
+def flat(spot, dims):
+    return (spot[0] * dims[1] + spot[1]) * dims[2] + spot[2]
+
+
+def targets_of(spots, dims):
+    nx, ny, nz = dims
+    half = nz // 2 if nz % 2 == 0 else nz
+    side = spots[2] // half
+    sides = nz // half
+    targets = []
+    for s in range(1, sides + 1):
+        base = wrapped(side + s, sides) * half
+        for c in range(half):
+            for a in range(nx):
+                for b in range(ny):
+                    spot = (wrapped(spots[0] + a, nx), wrapped(spots[1] + b, ny), base + c)
+                    targets.append((spot, s == sides and a == 0 and b == 0))
+    return targets
 
 
 def exchange_kernel(
@@ -64,18 +83,18 @@
     nx, ny, nz = dims
     devices = nx * ny * nz
     spots = [lax.axis_index(axis) for axis in AXES]
-    me = (spots[0] * ny + spots[1]) * nz + spots[2]
+    me = flat(spots, dims)
     ring = [[wrapped(spot + k, size) for k in range(size)] for spot, size in zip(spots, dims)]
     rows, width = held.shape
     chunk = rows // chunks
     halves = width // LANES
-    sent_rows = fields_at + 2
-    steps = steps_of(dims)
+    sent_rows = fields_at + 1
+    steps = relative_steps(dims)
 
     count_load = pltpu.make_async_copy(count_hbm, count_ref, small_sem.at[0])
     count_load.start()
     barrier = pltpu.get_barrier_semaphore()
-    for _, k in steps:
+    for k in steps:
         pl.semaphore_signal(
             barrier, inc=1, device_id=tuple(r[i] for r, i in zip(ring, k)), device_id_type=MESH
         )
@@ -90,24 +109,23 @@
     keys_load = pltpu.make_async_copy(keys_hbm, keys_ref, small_sem.at[2])
     keys_load.start()
 
-    def remote(source, goal, sems, k):
+    def remote(source, goal, sems, spot):
         return pltpu.make_async_remote_copy(
             src_ref=source,
             dst_ref=goal,
             send_sem=sems.at[0],
             recv_sem=sems.at[1],
-            device_id=tuple(r[i] for r, i in zip(ring, k)),
+            device_id=tuple(spot),
             device_id_type=MESH,
         )
 
     count_load.wait()
-    cbuf[0] = jnp.broadcast_to(count_ref[...], cbuf.shape[1:])
+    cbuf[me] = jnp.full(cbuf.shape[1:], count_ref[0], jnp.int32)
     index_load.wait()
 
     row = lax.broadcasted_iota(jnp.int32, (span, LANES), 0)
     labels = lax.rem(row, levels) * devices + row // levels
 
-    total = None
     for c in range(chunks):
         loads[c].wait()
         x = held[pl.ds(c * chunk, chunk), :]
@@ -133,15 +151,15 @@
                 stage[:, h * levels : (h + 1) * levels, :] += block
         if c == 0:
             pl.semaphore_wait(barrier, devices - 1)
-            for slot, k in steps:
-                remote(cbuf.at[0], cbuf.at[slot], count_sem, k).start()
+            for k in steps:
+                remote(cbuf.at[me], cbuf.at[me], count_sem, [r[i] for r, i in zip(ring, k)]).start()
 
     tallies = lax.dot_general(
         jnp.ones((8, LANES), jnp.bfloat16),
         tally_ref[...].astype(jnp.bfloat16),
         (((1,), (1,)), ((), ())),
         preferred_element_type=jnp.float32,
-    )[0:1]
+    )
     keys_load.wait()
     keys = keys_ref[...]
     source = lax.broadcasted_iota(jnp.int32, (span, span), 0)
@@ -156,33 +174,39 @@
         pieces.astype(jnp.float32).astype(jnp.bfloat16), moved, preferred_element_type=jnp.float32
     )
     placed = pieces[0:1] + pieces[1:2] * 256.0 + pieces[2:3] * 65536.0
-    fields = jnp.concatenate([tallies, placed], axis=0)
-    for a in range(devices):
-        tile = a * levels // LANES * LANES
-        stage[a, fields_at : fields_at + 2, :] = fields[:, tile : tile + LANES]
+    lane = lax.broadcasted_iota(jnp.int32, (1, LANES), 1)
+    for t in range(span // LANES):
+        tile = slice(t * LANES, (t + 1) * LANES)
+        keyed = pltpu.roll(jnp.broadcast_to(placed[:, tile], (8, LANES)), LANES // 2, 1)[0:1]
+        counted = tallies[0:1, tile]
+        lows = jnp.where(lane < LANES // 2, counted, keyed)
+        highs = jnp.where(lane < LANES // 2, keyed, counted)
+        for a in range(t * LANES // levels, (t + 1) * LANES // levels):
+            within = a * levels % LANES
+            stage[a, fields_at : fields_at + 1, :] = lows if within < LANES // 2 else highs
 
     others = cbuf.at[pl.ds(1, devices - 1)]
     pltpu.make_async_copy(others, others, count_sem.at[1]).wait()
     counts = cbuf[...][:, 0, :]
-    slots = lax.broadcasted_iota(jnp.int32, counts.shape, 0)
-    parts = (divide(slots, ny * nz), modulo(divide(slots, nz), ny), modulo(slots, nz))
-    back = [
-        jnp.where(spot >= part, spot - part, spot - part + size)
-        for spot, part, size in zip(spots, parts, dims)
-    ]
-    sender = (back[0] * ny + back[1]) * nz + back[2]
-    lane = lax.broadcasted_iota(jnp.int32, counts.shape, 1)
-    counts_ref[...] = jnp.sum(jnp.where(sender == lane, counts, 0), axis=0, keepdims=True)
+    sender = lax.broadcasted_iota(jnp.int32, counts.shape, 0)
+    place = lax.broadcasted_iota(jnp.int32, counts.shape, 1)
     before = jnp.sum(jnp.where(sender < me, counts, 0), axis=0, keepdims=True)[0, 0]
     shift = modulo(before, devices)
 
-    for slot, (a, b, c) in steps:
-        other = (ring[0][a] * ny + ring[1][b]) * nz + ring[2][c]
-        send[slot] = stage[modulo(other - shift + devices, devices)]
-    for slot, k in steps:
-        piece = pl.ds(0, sent_rows)
-        remote(send.at[slot, piece], recv_ref.at[slot, piece], data_sem, k).start()
-    recv_ref[0] = stage[modulo(me - shift + devices, devices)]
+    targets = targets_of(spots, dims)
+    for spot, _ in targets:
+        other = flat(spot, dims)
+        send[other] = stage[modulo(other - shift + devices, devices)]
+    piece = pl.ds(0, sent_rows)
+    for spot, maybe in targets:
+        other = flat(spot, dims)
+        copy = remote(send.at[other, piece], recv_ref.at[me, piece], data_sem, spot)
+        if maybe:
+            pl.when(other != me)(copy.start)
+        else:
+            copy.start()
+    recv_ref[me] = send[me]
+    counts_ref[...] = jnp.sum(jnp.where(sender == place, counts, 0), axis=0, keepdims=True)
     pltpu.make_async_copy(others, others, count_sem.at[0]).wait()
     landed = recv_ref.at[pl.ds(1, devices - 1), pl.ds(0, sent_rows)]
     left = send.at[pl.ds(1, devices - 1), pl.ds(0, sent_rows)]
@@ -198,25 +222,24 @@
     devices = nx * ny * nz
     spots = [lax.axis_index(axis) for axis in AXES]
     me = (spots[0] * ny + spots[1]) * nz + spots[2]
-    back = [
-        [jnp.where(spot >= k, spot - k, spot - k + size) for k in range(size)]
-        for spot, size in zip(spots, dims)
-    ]
     halves = sums_ref.shape[1] // LANES
     lane = lax.broadcasted_iota(jnp.int32, (8, span), 1)
     fields = jnp.zeros((8, span), jnp.float32)
+    keyed = fields
     offset = jnp.int32(0)
 
     for d in range(devices):
-        slot = (back[0][d // (ny * nz)] * ny + back[1][d // nz % ny]) * nz + back[2][d % nz]
         first = modulo(me - modulo(offset, devices) + devices, devices)
         start = divide(offset + first, devices)
         for h in range(halves):
-            buf[h, pl.ds(start, levels), :] = recv_ref[slot, h * levels : (h + 1) * levels, :]
+            buf[h, pl.ds(start, levels), :] = recv_ref[d, h * levels : (h + 1) * levels, :]
         turn = modulo(modulo(start, LANES) - modulo(first * levels, LANES) + LANES, LANES)
-        turned = pltpu.roll(recv_ref[slot, fields_at : fields_at + 8, :], turn, 1)
+        turned = pltpu.roll(recv_ref[d, fields_at : fields_at + 8, :], turn, 1)
         wide = jnp.concatenate([turned] * (span // LANES), axis=1)
         fields = jnp.where(lane >= start, wide, fields)
+        turned = pltpu.roll(turned, LANES // 2, 1)
+        wide = jnp.concatenate([turned] * (span // LANES), axis=1)
+        keyed = jnp.where(lane >= start, wide, keyed)
         offset = offset + counts_ref[0, d]
 
     total_ref[0, 0] = offset
@@ -226,7 +249,7 @@
         sums_ref[:, h * LANES : (h + 1) * LANES] = jnp.where(row < taken, buf[h, 0:span, :], 0.0)
     inside = lane[0:1] < taken
     rows_ref[...] = jnp.where(inside, fields[0:1].astype(jnp.int32), 0)
-    keys_ref[...] = jnp.where(inside, fields[1:2].astype(jnp.int32), -1)
+    keys_ref[...] = jnp.where(inside, keyed[0:1].astype(jnp.int32), -1)
 
 
 def shards(measures, group_index, distinct_keys, group_counts):
@@ -236,8 +259,8 @@
     devices = dims[0] * dims[1] * dims[2]
     levels = span // devices
     chunks = 4 if rows % (4 * LANES) == 0 else 1
-    fields_at = round_up(levels * (width // LANES), 8)
-    slab = fields_at + 8
+    fields_at = levels * (width // LANES)
+    slab = round_up(fields_at + 8, 8)
     wide = round_up(devices, LANES)
     vmem = pl.BlockSpec(memory_space=pltpu.VMEM)
     smem = pl.BlockSpec(memory_space=pltpu.SMEM)
@@ -260,7 +283,7 @@
             pltpu.VMEM((devices, 1, wide), jnp.int32),
             pltpu.VMEM((rows // LANES, LANES), jnp.int32),
             pltpu.VMEM((1, span), jnp.int32),
-            pltpu.VMEM((1, 1), jnp.int32),
+            pltpu.SMEM((1,), jnp.int32),
             pltpu.SemaphoreType.DMA((3,)),
             pltpu.SemaphoreType.DMA((chunks,)),
             pltpu.SemaphoreType.DMA((2,)),
@@ -268,7 +291,7 @@
         ],
         compiler_params=pltpu.CompilerParams(collective_id=0, has_side_effects=True),
         name="exchange",
-    )(group_index.reshape(rows // LANES, LANES), distinct_keys, group_counts.reshape(1, 1), measures)
+    )(group_index.reshape(rows // LANES, LANES), distinct_keys, group_counts, measures)
     sums, tallies, keys, total = pl.pallas_call(
         functools.partial(place_kernel, (dims, span, levels, fields_at)),
         out_shape=(

time: 26.1 us -> 25.9 us (level)
    pallas_call x1, Pallas kernels: 22.9 us -> 22.6 us  [shards(): pl.pallas_call(functools.partial(exchange_kernel, (dims, span, levels, ch...]
where the time goes in v1:
time: 25.9 us; the launch traced here: 25.5 us
  Pallas kernels  24.3 us (94%)
  between operations  1.29 us (5%)
    pallas_call x1, Pallas kernels, shards(): pl.pallas_call(functools.partial(exchange_kernel, (dims, span, levels, ch...  22.6 us
    pallas_call x1, Pallas kernels, shards(): pl.pallas_call(functools.partial(place_kernel, (dims, span, levels, field...  1.65 us

profile of v1, /device:TPU:13, one launch (start us, length us, event | category | flops | bytes accessed | tf_op | source)
XLA Modules:
  0.0 25.5 jit_solution(5832405276835574274)
XLA Ops:
  1.3 22.6 %exchange.1 = (f32[32,40,128]{2,1,0:T(8,128)S(1)}, s32[1,128]{1,0:T(1,128)S(1)}) custom-call(s32[16,128]{1,0:T(8,128)} %bitcast.4, s32[1,512]{1,0:T(1,128)} %keys_hbm.1, s32[1]{0:T(128)S(6)} %copy.8.count_hbm, f32[2048,256]{1,0:T(8,128)} %measures_ref.1), custom_call_target="tpu_custom_call" | custom-call | tf_op jit(solution)/shard_map/exchange/pallas_call | solution.py:268
  23.9 1.7 %place.1 = (f32[512,256]{1,0:T(8,128)}, s32[1,512]{1,0:T(1,128)}, s32[1,512]{1,0:T(1,128)}, s32[1,1]{1,0:T(1,128)}) custom-call(s32[1,128]{1,0:T(1,128)S(1)} %get-tuple-element.10.counts_ref, f32[32,40,128]{2,1,0:T(8,128)S(1)} %get-tuple-element.11.recv_ref), custom_call_target="tpu_custom_call" | custom-call | tf_op jit(solution)/shard_map/place/pallas_call | solution.py:295

commit v2 on v1

--- a/solution.py
+++ b/solution.py
@@ -14,12 +14,6 @@
 
 def round_up(value, unit):
     return (value + unit - 1) // unit * unit
-
-
-def relative_steps(dims):
-    nx, ny, nz = dims
-    steps = [(a, b, c) for c in range(nz) for a in range(nx) for b in range(ny)]
-    return [k for k in steps if k != (0, 0, 0)]
 
 
 def wrapped(value, size):
@@ -62,7 +56,6 @@
     shape,
     index_hbm,
     keys_hbm,
-    count_hbm,
     measures_ref,
     recv_ref,
     counts_ref,
@@ -73,7 +66,7 @@
     cbuf,
     index_ref,
     keys_ref,
-    count_ref,
+    mate_ref,
     small_sem,
     load_sem,
     count_sem,
@@ -89,17 +82,32 @@
     chunk = rows // chunks
     halves = width // LANES
     sent_rows = fields_at + 1
-    steps = relative_steps(dims)
-
-    count_load = pltpu.make_async_copy(count_hbm, count_ref, small_sem.at[0])
-    count_load.start()
-    barrier = pltpu.get_barrier_semaphore()
-    for k in steps:
-        pl.semaphore_signal(
-            barrier, inc=1, device_id=tuple(r[i] for r, i in zip(ring, k)), device_id_type=MESH
-        )
+
     index_load = pltpu.make_async_copy(index_hbm, index_ref, small_sem.at[1])
     index_load.start()
+    cores = 2 if ny % 2 == 0 else 1
+    core = modulo(spots[1], cores)
+    leads = core == cores - 1
+    pairs = ny // cores
+    chips = nx * pairs * nz
+    pair = divide(spots[1], cores)
+    chip = (spots[0] * pairs + pair) * nz + spots[2]
+    mate = (spots[0], spots[1] + 1 - 2 * core, spots[2])
+    leaders, followers = [], []
+    for a in range(nx):
+        for b in range(pairs):
+            for c in range(nz):
+                spot = [ring[0][a], wrapped(pair + b, pairs) * cores, ring[2][c]]
+                if (a, b, c) != (0, 0, 0):
+                    leaders.append((spot[0], spot[1] + cores - 1, spot[2]))
+                    if cores == 2:
+                        followers.append(tuple(spot))
+
+    barrier = pltpu.get_barrier_semaphore()
+    if cores == 2:
+        pl.semaphore_signal(barrier, inc=1, device_id=mate, device_id_type=MESH)
+    for spot in leaders:
+        pl.semaphore_signal(barrier, inc=1, device_id=spot, device_id_type=MESH)
     loads = []
     for c in range(chunks):
         piece = pl.ds(c * chunk, chunk)
@@ -119,9 +127,38 @@
             device_id_type=MESH,
         )
 
-    count_load.wait()
-    cbuf[me] = jnp.full(cbuf.shape[1:], count_ref[0], jnp.int32)
     index_load.wait()
+    top = jnp.max(index_ref[...], axis=0, keepdims=True)
+    mine = jnp.broadcast_to(jnp.max(top, axis=1, keepdims=True) + 1, cbuf.shape[1:])
+    lane = lax.broadcasted_iota(jnp.int32, cbuf.shape[1:], 1)
+    wide_chip = divide(lane, cores * nz) * nz + modulo(lane, nz)
+    wide_core = modulo(divide(lane, nz), cores)
+    cbuf[chip] = mine
+
+    def tell_mate():
+        pl.semaphore_wait(barrier, 1)
+        mate_copy.start()
+
+    def tell_all():
+        pl.semaphore_wait(barrier, devices - 1)
+        if cores == 2:
+            mate_copy.wait_recv()
+            cbuf[chip] = jnp.where(wide_core == core, mine, mate_ref[1])
+            remote(cbuf.at[chip], cbuf.at[chip], count_sem, mate).start()
+        for spot in leaders + followers:
+            remote(cbuf.at[chip], cbuf.at[chip], count_sem, spot).start()
+
+    if cores == 2:
+        mate_ref[0] = mine
+        mate_copy = pltpu.make_async_remote_copy(
+            src_ref=mate_ref.at[0],
+            dst_ref=mate_ref.at[1],
+            send_sem=small_sem.at[0],
+            recv_sem=small_sem.at[3],
+            device_id=mate,
+            device_id_type=MESH,
+        )
+        pl.when(jnp.logical_not(leads))(tell_mate)
 
     row = lax.broadcasted_iota(jnp.int32, (span, LANES), 0)
     labels = lax.rem(row, levels) * devices + row // levels
@@ -150,9 +187,7 @@
             else:
                 stage[:, h * levels : (h + 1) * levels, :] += block
         if c == 0:
-            pl.semaphore_wait(barrier, devices - 1)
-            for k in steps:
-                remote(cbuf.at[me], cbuf.at[me], count_sem, [r[i] for r, i in zip(ring, k)]).start()
+            pl.when(leads)(tell_all)
 
     tallies = lax.dot_general(
         jnp.ones((8, LANES), jnp.bfloat16),
@@ -174,23 +209,31 @@
         pieces.astype(jnp.float32).astype(jnp.bfloat16), moved, preferred_element_type=jnp.float32
     )
     placed = pieces[0:1] + pieces[1:2] * 256.0 + pieces[2:3] * 65536.0
-    lane = lax.broadcasted_iota(jnp.int32, (1, LANES), 1)
+    line = lax.broadcasted_iota(jnp.int32, (1, LANES), 1)
     for t in range(span // LANES):
         tile = slice(t * LANES, (t + 1) * LANES)
         keyed = pltpu.roll(jnp.broadcast_to(placed[:, tile], (8, LANES)), LANES // 2, 1)[0:1]
         counted = tallies[0:1, tile]
-        lows = jnp.where(lane < LANES // 2, counted, keyed)
-        highs = jnp.where(lane < LANES // 2, keyed, counted)
+        lows = jnp.where(line < LANES // 2, counted, keyed)
+        highs = jnp.where(line < LANES // 2, keyed, counted)
         for a in range(t * LANES // levels, (t + 1) * LANES // levels):
             within = a * levels % LANES
             stage[a, fields_at : fields_at + 1, :] = lows if within < LANES // 2 else highs
 
-    others = cbuf.at[pl.ds(1, devices - 1)]
-    pltpu.make_async_copy(others, others, count_sem.at[1]).wait()
-    counts = cbuf[...][:, 0, :]
-    sender = lax.broadcasted_iota(jnp.int32, counts.shape, 0)
-    place = lax.broadcasted_iota(jnp.int32, counts.shape, 1)
-    before = jnp.sum(jnp.where(sender < me, counts, 0), axis=0, keepdims=True)[0, 0]
+    def await_others():
+        others = cbuf.at[pl.ds(1, chips - 1)]
+        pltpu.make_async_copy(others, others, count_sem.at[1]).wait()
+
+    def await_all():
+        pltpu.make_async_copy(cbuf, cbuf, count_sem.at[1]).wait()
+
+    pl.when(leads)(await_others)
+    if cores == 2:
+        pl.when(jnp.logical_not(leads))(await_all)
+    shown = cbuf[...][:, 0, :]
+    place = lax.broadcasted_iota(jnp.int32, shown.shape, 0)
+    counts = jnp.sum(jnp.where(place == wide_chip, shown, 0), axis=0, keepdims=True)
+    before = jnp.sum(jnp.where(lane < me, counts, 0))
     shift = modulo(before, devices)
 
     targets = targets_of(spots, dims)
@@ -206,8 +249,17 @@
         else:
             copy.start()
     recv_ref[me] = send[me]
-    counts_ref[...] = jnp.sum(jnp.where(sender == place, counts, 0), axis=0, keepdims=True)
-    pltpu.make_async_copy(others, others, count_sem.at[0]).wait()
+    counts_ref[...] = counts
+
+    def sent_counts():
+        told = cbuf.at[pl.ds(1, chips - 1)]
+        pltpu.make_async_copy(told, told, count_sem.at[0]).wait()
+        if cores == 2:
+            pltpu.make_async_copy(cbuf, cbuf, count_sem.at[0]).wait()
+
+    pl.when(leads)(sent_counts)
+    if cores == 2:
+        pl.when(jnp.logical_not(leads))(mate_copy.wait_send)
     landed = recv_ref.at[pl.ds(1, devices - 1), pl.ds(0, sent_rows)]
     left = send.at[pl.ds(1, devices - 1), pl.ds(0, sent_rows)]
     pltpu.make_async_copy(left, left, data_sem.at[0]).wait()
@@ -262,6 +314,7 @@
     fields_at = levels * (width // LANES)
     slab = round_up(fields_at + 8, 8)
     wide = round_up(devices, LANES)
+    cores = 2 if dims[1] % 2 == 0 else 1
     vmem = pl.BlockSpec(memory_space=pltpu.VMEM)
     smem = pl.BlockSpec(memory_space=pltpu.SMEM)
     anywhere = pl.BlockSpec(memory_space=pl.ANY)
@@ -273,25 +326,25 @@
             pltpu.VMEM((devices, slab, LANES), jnp.float32),
             pltpu.VMEM((1, wide), jnp.int32),
         ),
-        in_specs=[anywhere] * 4,
+        in_specs=[anywhere] * 3,
         out_specs=(vmem, vmem),
         scratch_shapes=[
             pltpu.VMEM((rows, width), jnp.float32),
             pltpu.VMEM((devices, slab, LANES), jnp.float32),
             pltpu.VMEM((devices, slab, LANES), jnp.float32),
             pltpu.VMEM((span, LANES), jnp.float32),
-            pltpu.VMEM((devices, 1, wide), jnp.int32),
+            pltpu.VMEM((devices // cores, 1, wide), jnp.int32),
             pltpu.VMEM((rows // LANES, LANES), jnp.int32),
             pltpu.VMEM((1, span), jnp.int32),
-            pltpu.SMEM((1,), jnp.int32),
-            pltpu.SemaphoreType.DMA((3,)),
+            pltpu.VMEM((2, 1, wide), jnp.int32),
+            pltpu.SemaphoreType.DMA((4,)),
             pltpu.SemaphoreType.DMA((chunks,)),
             pltpu.SemaphoreType.DMA((2,)),
             pltpu.SemaphoreType.DMA((2,)),
         ],
         compiler_params=pltpu.CompilerParams(collective_id=0, has_side_effects=True),
         name="exchange",
-    )(group_index.reshape(rows // LANES, LANES), distinct_keys, group_counts, measures)
+    )(group_index.reshape(rows // LANES, LANES), distinct_keys, measures)
     sums, tallies, keys, total = pl.pallas_call(
         functools.partial(place_kernel, (dims, span, levels, fields_at)),
         out_shape=(

time: 25.9 us -> 24.8 us (0.958)
  between operations: 1.29 us -> 0.64 us
  Pallas kernels: 24.3 us -> 23.7 us
    pallas_call x1, Pallas kernels: 22.6 us -> 22.1 us  [shards(): pl.pallas_call(functools.partial(exchange_kernel, (dims, span, levels, ch...]
where the time goes in v2:
time: 24.8 us; the launch traced here: 24.3 us
  Pallas kernels  23.7 us (96%)
  between operations  0.64 us (3%)
    pallas_call x1, Pallas kernels, shards(): pl.pallas_call(functools.partial(exchange_kernel, (dims, span, levels, ch...  22.1 us
    pallas_call x1, Pallas kernels, shards(): pl.pallas_call(functools.partial(place_kernel, (dims, span, levels, field...  1.65 us

profile of v2, /device:TPU:13, one launch (start us, length us, event | category | flops | bytes accessed | tf_op | source)
XLA Modules:
  0.0 24.3 jit_solution(15518956574168997649)
XLA Ops:
  0.6 22.1 %exchange.1 = (f32[32,40,128]{2,1,0:T(8,128)S(1)}, s32[1,128]{1,0:T(1,128)S(1)}) custom-call(s32[16,128]{1,0:T(8,128)} %bitcast.4, s32[1,512]{1,0:T(1,128)} %keys_hbm.1, f32[2048,256]{1,0:T(8,128)} %measures_ref.1), custom_call_target="tpu_custom_call" | custom-call | tf_op jit(solution)/shard_map/exchange/pallas_call | solution.py:321
  22.7 1.7 %place.1 = (f32[512,256]{1,0:T(8,128)}, s32[1,512]{1,0:T(1,128)}, s32[1,512]{1,0:T(1,128)}, s32[1,1]{1,0:T(1,128)}) custom-call(s32[1,128]{1,0:T(1,128)S(1)} %get-tuple-element.10.counts_ref, f32[32,40,128]{2,1,0:T(8,128)S(1)} %get-tuple-element.11.recv_ref), custom_call_target="tpu_custom_call" | custom-call | tf_op jit(solution)/shard_map/place/pallas_call | solution.py:348

commit v3 on v2

--- a/solution.py
+++ b/solution.py
@@ -39,16 +39,15 @@
 def targets_of(spots, dims):
     nx, ny, nz = dims
     half = nz // 2 if nz % 2 == 0 else nz
+    sides = nz // half
     side = spots[2] // half
-    sides = nz // half
     targets = []
     for s in range(1, sides + 1):
         base = wrapped(side + s, sides) * half
         for c in range(half):
             for a in range(nx):
                 for b in range(ny):
-                    spot = (wrapped(spots[0] + a, nx), wrapped(spots[1] + b, ny), base + c)
-                    targets.append((spot, s == sides and a == 0 and b == 0))
+                    targets.append(((jnp.int32(a), jnp.int32(b), base + c), s == sides))
     return targets
 
 
@@ -67,6 +66,7 @@
     index_ref,
     keys_ref,
     mate_ref,
+    counts_kept,
     small_sem,
     load_sem,
     count_sem,
@@ -237,19 +237,24 @@
     shift = modulo(before, devices)
 
     targets = targets_of(spots, dims)
-    for spot, _ in targets:
-        other = flat(spot, dims)
-        send[other] = stage[modulo(other - shift + devices, devices)]
     piece = pl.ds(0, sent_rows)
-    for spot, maybe in targets:
-        other = flat(spot, dims)
-        copy = remote(send.at[other, piece], recv_ref.at[me, piece], data_sem, spot)
-        if maybe:
-            pl.when(other != me)(copy.start)
-        else:
-            copy.start()
+    for across in (False, True) if any(not own for _, own in targets) else (True,):
+        for spot, own in targets:
+            if own == across:
+                other = flat(spot, dims)
+                send[other] = stage[modulo(other - shift + devices, devices)]
+        for spot, own in targets:
+            if own == across:
+                other = flat(spot, dims)
+                copy = remote(send.at[other, piece], recv_ref.at[me, piece], data_sem, spot)
+                if own:
+                    pl.when(other != me)(copy.start)
+                else:
+                    copy.start()
     recv_ref[me] = send[me]
-    counts_ref[...] = counts
+    counts_kept[...] = counts
+    counts_copy = pltpu.make_async_copy(counts_kept, counts_ref, small_sem.at[4])
+    counts_copy.start()
 
     def sent_counts():
         told = cbuf.at[pl.ds(1, chips - 1)]
@@ -264,44 +269,71 @@
     left = send.at[pl.ds(1, devices - 1), pl.ds(0, sent_rows)]
     pltpu.make_async_copy(left, left, data_sem.at[0]).wait()
     pltpu.make_async_copy(landed, landed, data_sem.at[1]).wait()
+    counts_copy.wait()
 
 
 def place_kernel(
-    shape, counts_ref, recv_ref, sums_ref, rows_ref, keys_ref, total_ref, buf
+    shape,
+    counts_ref,
+    recv_ref,
+    sums_ref,
+    rows_ref,
+    keys_ref,
+    total_ref,
+    buf,
+    row_line,
+    key_line,
+    total_line,
+    sems,
 ):
     dims, span, levels, fields_at = shape
     nx, ny, nz = dims
     devices = nx * ny * nz
     spots = [lax.axis_index(axis) for axis in AXES]
-    me = (spots[0] * ny + spots[1]) * nz + spots[2]
-    halves = sums_ref.shape[1] // LANES
-    lane = lax.broadcasted_iota(jnp.int32, (8, span), 1)
-    fields = jnp.zeros((8, span), jnp.float32)
-    keyed = fields
+    me = flat(spots, dims)
+    halves = buf.shape[0]
+
+    for h in range(halves):
+        buf[h] = jnp.zeros(buf.shape[1:], jnp.float32)
     offset = jnp.int32(0)
-
+    starts, turns = [], []
     for d in range(devices):
         first = modulo(me - modulo(offset, devices) + devices, devices)
         start = divide(offset + first, devices)
         for h in range(halves):
             buf[h, pl.ds(start, levels), :] = recv_ref[d, h * levels : (h + 1) * levels, :]
-        turn = modulo(modulo(start, LANES) - modulo(first * levels, LANES) + LANES, LANES)
-        turned = pltpu.roll(recv_ref[d, fields_at : fields_at + 8, :], turn, 1)
-        wide = jnp.concatenate([turned] * (span // LANES), axis=1)
-        fields = jnp.where(lane >= start, wide, fields)
-        turned = pltpu.roll(turned, LANES // 2, 1)
-        wide = jnp.concatenate([turned] * (span // LANES), axis=1)
-        keyed = jnp.where(lane >= start, wide, keyed)
+        starts.append(start)
+        turns.append(modulo(start - first * levels + span, LANES))
         offset = offset + counts_ref[0, d]
-
-    total_ref[0, 0] = offset
+    copies = []
+    for h in range(halves):
+        copies.append(
+            pltpu.make_async_copy(
+                buf.at[h, pl.ds(0, span)], sums_ref.at[:, pl.ds(h * LANES, LANES)], sems.at[h]
+            )
+        )
+        copies[-1].start()
+
+    total_line[0, 0] = offset
+    copies.append(pltpu.make_async_copy(total_line, total_ref, sems.at[halves]))
+    copies[-1].start()
     taken = divide(offset - me + devices - 1, devices)
-    row = lax.broadcasted_iota(jnp.int32, (span, LANES), 0)
-    for h in range(halves):
-        sums_ref[:, h * LANES : (h + 1) * LANES] = jnp.where(row < taken, buf[h, 0:span, :], 0.0)
+    lane = lax.broadcasted_iota(jnp.int32, (8, span), 1)
+    counted = jnp.zeros((8, span), jnp.float32)
+    keyed = counted
+    for d in range(devices):
+        turned = pltpu.roll(recv_ref[d, fields_at : fields_at + 8, :], turns[d], 1)
+        other = pltpu.roll(turned, LANES // 2, 1)
+        counted = jnp.where(lane >= starts[d], jnp.concatenate([turned] * (span // LANES), 1), counted)
+        keyed = jnp.where(lane >= starts[d], jnp.concatenate([other] * (span // LANES), 1), keyed)
     inside = lane[0:1] < taken
-    rows_ref[...] = jnp.where(inside, fields[0:1].astype(jnp.int32), 0)
-    keys_ref[...] = jnp.where(inside, keyed[0:1].astype(jnp.int32), -1)
+    row_line[...] = jnp.where(inside, counted[0:1].astype(jnp.int32), 0)
+    key_line[...] = jnp.where(inside, keyed[0:1].astype(jnp.int32), -1)
+    for k, (line, goal) in enumerate(((row_line, rows_ref), (key_line, keys_ref))):
+        copies.append(pltpu.make_async_copy(line, goal, sems.at[halves + 1 + k]))
+        copies[-1].start()
+    for copy in copies:
+        copy.wait()
 
 
 def shards(measures, group_index, distinct_keys, group_counts):
@@ -324,10 +356,10 @@
         ),
         out_shape=(
             pltpu.VMEM((devices, slab, LANES), jnp.float32),
-            pltpu.VMEM((1, wide), jnp.int32),
+            pltpu.SMEM((1, wide), jnp.int32),
         ),
         in_specs=[anywhere] * 3,
-        out_specs=(vmem, vmem),
+        out_specs=(vmem, smem),
         scratch_shapes=[
             pltpu.VMEM((rows, width), jnp.float32),
             pltpu.VMEM((devices, slab, LANES), jnp.float32),
@@ -337,7 +369,8 @@
             pltpu.VMEM((rows // LANES, LANES), jnp.int32),
             pltpu.VMEM((1, span), jnp.int32),
             pltpu.VMEM((2, 1, wide), jnp.int32),
-            pltpu.SemaphoreType.DMA((4,)),
+            pltpu.VMEM((1, wide), jnp.int32),
+            pltpu.SemaphoreType.DMA((5,)),
             pltpu.SemaphoreType.DMA((chunks,)),
             pltpu.SemaphoreType.DMA((2,)),
             pltpu.SemaphoreType.DMA((2,)),
@@ -354,11 +387,20 @@
             jax.ShapeDtypeStruct((1, 1), jnp.int32),
         ),
         in_specs=[smem, vmem],
-        out_specs=(vmem, vmem, vmem, smem),
-        scratch_shapes=[pltpu.VMEM((width // LANES, span + round_up(levels, 8), LANES), jnp.float32)],
+        out_specs=(anywhere,) * 4,
+        scratch_shapes=[
+            pltpu.VMEM((width // LANES, span + round_up(levels, 8), LANES), jnp.float32),
+            pltpu.VMEM((1, span), jnp.int32),
+            pltpu.VMEM((1, span), jnp.int32),
+            pltpu.SMEM((1, 1), jnp.int32),
+            pltpu.SemaphoreType.DMA((width // LANES + 3,)),
+        ],
         compiler_params=pltpu.CompilerParams(vmem_limit_bytes=16 * 1024 * 1024),
         name="place",
-    )(*(pltpu.with_memory_space_constraint(part, pltpu.VMEM) for part in (counts, received)))
+    )(
+        pltpu.with_memory_space_constraint(counts, pltpu.SMEM),
+        pltpu.with_memory_space_constraint(received, pltpu.VMEM),
+    )
     return sums, tallies.reshape(span), keys.reshape(span), total.reshape(())
 
 

time: 24.8 us -> 23.6 us (0.952); the launches traced: 24.3 us -> 23.4 us
  Pallas kernels: 23.7 us -> 22.8 us
    pallas_call x1, Pallas kernels: 1.65 us -> 1.04 us  [shards(): pl.pallas_call(functools.partial(place_kernel, (dims, span, levels, field...]
    pallas_call x1, Pallas kernels: 22.1 us -> 21.7 us  [shards(): pl.pallas_call(functools.partial(exchange_kernel, (dims, span, levels, ch...]
where the time goes in v3:
time: 23.6 us; the launch traced here: 23.4 us
  Pallas kernels  22.8 us (97%)
  between operations  0.64 us (3%)
    pallas_call x1, Pallas kernels, shards(): pl.pallas_call(functools.partial(exchange_kernel, (dims, span, levels, ch...  21.7 us
    pallas_call x1, Pallas kernels, shards(): pl.pallas_call(functools.partial(place_kernel, (dims, span, levels, field...  1.04 us

profile of v3, /device:TPU:13, one launch (start us, length us, event | category | flops | bytes accessed | tf_op | source)
XLA Modules:
  0.0 23.4 jit_solution(9896218115895336545)
XLA Ops:
  0.6 21.7 %exchange.1 = (f32[32,40,128]{2,1,0:T(8,128)S(1)}, s32[1,128]{1,0:T(1,128)S(4)}) custom-call(s32[16,128]{1,0:T(8,128)} %bitcast.4, s32[1,512]{1,0:T(1,128)} %keys_hbm.1, f32[2048,256]{1,0:T(8,128)} %measures_ref.1), custom_call_target="tpu_custom_call" | custom-call | tf_op jit(solution)/shard_map/exchange/pallas_call | solution.py:353
  22.4 1.0 %place.1 = (f32[512,256]{1,0:T(8,128)}, s32[1,512]{1,0:T(1,128)}, s32[1,512]{1,0:T(1,128)}, s32[1,1]{1,0:T(1,128)}) custom-call(s32[1,128]{1,0:T(1,128)S(4)} %get-tuple-element.10.counts_ref, f32[32,40,128]{2,1,0:T(8,128)S(1)} %get-tuple-element.11.recv_ref), custom_call_target="tpu_custom_call" | custom-call | tf_op jit(solution)/shard_map/place/pallas_call | solution.py:381

commit v4 on v3

--- a/solution.py
+++ b/solution.py
@@ -71,6 +71,8 @@
     load_sem,
     count_sem,
     data_sem,
+    row_sem,
+    above_sem,
 ):
     dims, span, levels, chunks, fields_at = shape
     nx, ny, nz = dims
@@ -88,26 +90,37 @@
     cores = 2 if ny % 2 == 0 else 1
     core = modulo(spots[1], cores)
     leads = core == cores - 1
+    follows = jnp.logical_not(leads)
     pairs = ny // cores
-    chips = nx * pairs * nz
+    plane = nx * pairs
+    chips = plane * nz
     pair = divide(spots[1], cores)
-    chip = (spots[0] * pairs + pair) * nz + spots[2]
-    mate = (spots[0], spots[1] + 1 - 2 * core, spots[2])
-    leaders, followers = [], []
-    for a in range(nx):
-        for b in range(pairs):
-            for c in range(nz):
-                spot = [ring[0][a], wrapped(pair + b, pairs) * cores, ring[2][c]]
-                if (a, b, c) != (0, 0, 0):
-                    leaders.append((spot[0], spot[1] + cores - 1, spot[2]))
-                    if cores == 2:
-                        followers.append(tuple(spot))
-
+    level = spots[2]
+    chip = level * plane + spots[0] * pairs + pair
+    mate = (spots[0], spots[1] + 1 - 2 * core, level)
+
+    def lead(a, b, z):
+        return (ring[0][a], wrapped(pair + b, pairs) * cores + cores - 1, z)
+
+    def planes(step, act):
+        for c in range(1, nz):
+            there = level + step * c
+            pl.when(there < nz if step > 0 else there >= 0)(functools.partial(act, there))
+
+    spread = [(a, b) for a in range(nx) for b in range(pairs)]
     barrier = pltpu.get_barrier_semaphore()
+
+    def greet(spot):
+        pl.semaphore_signal(barrier, inc=1, device_id=spot, device_id_type=MESH)
+
+    def greet_leads():
+        for a, b in spread[1:]:
+            greet(lead(a, b, level))
+        planes(1, lambda z: [greet(lead(a, b, z)) for a, b in spread] and None)
+
     if cores == 2:
-        pl.semaphore_signal(barrier, inc=1, device_id=mate, device_id_type=MESH)
-    for spot in leaders:
-        pl.semaphore_signal(barrier, inc=1, device_id=spot, device_id_type=MESH)
+        greet(mate)
+    pl.when(leads)(greet_leads)
     loads = []
     for c in range(chunks):
         piece = pl.ds(c * chunk, chunk)
@@ -117,48 +130,83 @@
     keys_load = pltpu.make_async_copy(keys_hbm, keys_ref, small_sem.at[2])
     keys_load.start()
 
-    def remote(source, goal, sems, spot):
+    def remote(source, goal, send_sem, recv_sem, spot):
         return pltpu.make_async_remote_copy(
             src_ref=source,
             dst_ref=goal,
-            send_sem=sems.at[0],
-            recv_sem=sems.at[1],
+            send_sem=send_sem,
+            recv_sem=recv_sem,
             device_id=tuple(spot),
             device_id_type=MESH,
         )
+
+    def take(ref, sem):
+        pltpu.make_async_copy(ref, ref, sem).wait()
 
     index_load.wait()
     top = jnp.max(index_ref[...], axis=0, keepdims=True)
     mine = jnp.broadcast_to(jnp.max(top, axis=1, keepdims=True) + 1, cbuf.shape[1:])
     lane = lax.broadcasted_iota(jnp.int32, cbuf.shape[1:], 1)
-    wide_chip = divide(lane, cores * nz) * nz + modulo(lane, nz)
+    wide_chip = modulo(lane, nz) * plane + divide(lane, cores * nz)
     wide_core = modulo(divide(lane, nz), cores)
-    cbuf[chip] = mine
 
     def tell_mate():
         pl.semaphore_wait(barrier, 1)
         mate_copy.start()
 
-    def tell_all():
-        pl.semaphore_wait(barrier, devices - 1)
+    def tell_leads():
+        pl.semaphore_wait(barrier, cores - 1 + plane - 1 + level * plane)
+        planes(
+            -1,
+            lambda z: pl.semaphore_signal(
+                above_sem, inc=1, device_id=lead(0, 0, z), device_id_type=MESH
+            ),
+        )
         if cores == 2:
             mate_copy.wait_recv()
             cbuf[chip] = jnp.where(wide_core == core, mine, mate_ref[1])
-            remote(cbuf.at[chip], cbuf.at[chip], count_sem, mate).start()
-        for spot in leaders + followers:
-            remote(cbuf.at[chip], cbuf.at[chip], count_sem, spot).start()
+        else:
+            cbuf[chip] = mine
+
+        def tell(z, some):
+            for a, b in some:
+                own = cbuf.at[chip]
+                remote(own, own, count_sem.at[0], row_sem.at[level], lead(a, b, z)).start()
+
+        tell(level, spread[1:])
+        planes(-1, lambda z: tell(z, spread))
+
+    def tell_above():
+        if plane > 1:
+            take(cbuf.at[pl.ds(0, plane - 1)], row_sem.at[level])
+        pl.when(level < nz - 1)(lambda: pl.semaphore_wait(above_sem, nz - 1 - level))
+        block = cbuf.at[pl.ds(level * plane, plane)]
+        planes(
+            1,
+            lambda z: remote(
+                block, block, count_sem.at[0], row_sem.at[level], lead(0, 0, z)
+            ).start(),
+        )
+
+    def hear_leads():
+        for step in (-1, 1):
+            planes(step, lambda z: take(cbuf.at[pl.ds(0, plane)], row_sem.at[z]))
+        if cores == 2:
+            remote(cbuf, cbuf, count_sem.at[0], count_sem.at[1], mate).start()
+
+    def hear_mate():
+        take(cbuf, count_sem.at[1])
+
+    def finish_leads():
+        if chips > 1:
+            take(cbuf.at[pl.ds(0, chips - 1)], count_sem.at[0])
+        if cores == 2:
+            take(cbuf, count_sem.at[0])
 
     if cores == 2:
         mate_ref[0] = mine
-        mate_copy = pltpu.make_async_remote_copy(
-            src_ref=mate_ref.at[0],
-            dst_ref=mate_ref.at[1],
-            send_sem=small_sem.at[0],
-            recv_sem=small_sem.at[3],
-            device_id=mate,
-            device_id_type=MESH,
-        )
-        pl.when(jnp.logical_not(leads))(tell_mate)
+        mate_copy = remote(mate_ref.at[0], mate_ref.at[1], small_sem.at[0], small_sem.at[3], mate)
+        pl.when(follows)(tell_mate)
 
     row = lax.broadcasted_iota(jnp.int32, (span, LANES), 0)
     labels = lax.rem(row, levels) * devices + row // levels
@@ -187,7 +235,8 @@
             else:
                 stage[:, h * levels : (h + 1) * levels, :] += block
         if c == 0:
-            pl.when(leads)(tell_all)
+            pl.when(leads)(tell_leads)
+    pl.when(leads)(tell_above)
 
     tallies = lax.dot_general(
         jnp.ones((8, LANES), jnp.bfloat16),
@@ -220,16 +269,9 @@
             within = a * levels % LANES
             stage[a, fields_at : fields_at + 1, :] = lows if within < LANES // 2 else highs
 
-    def await_others():
-        others = cbuf.at[pl.ds(1, chips - 1)]
-        pltpu.make_async_copy(others, others, count_sem.at[1]).wait()
-
-    def await_all():
-        pltpu.make_async_copy(cbuf, cbuf, count_sem.at[1]).wait()
-
-    pl.when(leads)(await_others)
+    pl.when(leads)(hear_leads)
     if cores == 2:
-        pl.when(jnp.logical_not(leads))(await_all)
+        pl.when(follows)(hear_mate)
     shown = cbuf[...][:, 0, :]
     place = lax.broadcasted_iota(jnp.int32, shown.shape, 0)
     counts = jnp.sum(jnp.where(place == wide_chip, shown, 0), axis=0, keepdims=True)
@@ -246,7 +288,13 @@
         for spot, own in targets:
             if own == across:
                 other = flat(spot, dims)
-                copy = remote(send.at[other, piece], recv_ref.at[me, piece], data_sem, spot)
+                copy = remote(
+                    send.at[other, piece],
+                    recv_ref.at[me, piece],
+                    data_sem.at[0],
+                    data_sem.at[1],
+                    spot,
+                )
                 if own:
                     pl.when(other != me)(copy.start)
                 else:
@@ -256,15 +304,9 @@
     counts_copy = pltpu.make_async_copy(counts_kept, counts_ref, small_sem.at[4])
     counts_copy.start()
 
-    def sent_counts():
-        told = cbuf.at[pl.ds(1, chips - 1)]
-        pltpu.make_async_copy(told, told, count_sem.at[0]).wait()
-        if cores == 2:
-            pltpu.make_async_copy(cbuf, cbuf, count_sem.at[0]).wait()
-
-    pl.when(leads)(sent_counts)
+    pl.when(leads)(finish_leads)
     if cores == 2:
-        pl.when(jnp.logical_not(leads))(mate_copy.wait_send)
+        pl.when(follows)(mate_copy.wait_send)
     landed = recv_ref.at[pl.ds(1, devices - 1), pl.ds(0, sent_rows)]
     left = send.at[pl.ds(1, devices - 1), pl.ds(0, sent_rows)]
     pltpu.make_async_copy(left, left, data_sem.at[0]).wait()
@@ -374,6 +416,8 @@
             pltpu.SemaphoreType.DMA((chunks,)),
             pltpu.SemaphoreType.DMA((2,)),
             pltpu.SemaphoreType.DMA((2,)),
+            pltpu.SemaphoreType.DMA((dims[2],)),
+            pltpu.SemaphoreType.REGULAR,
         ],
         compiler_params=pltpu.CompilerParams(collective_id=0, has_side_effects=True),
         name="exchange",

time: 23.6 us -> 23.1 us (0.979)
  Pallas kernels: 22.8 us -> 22.2 us
    pallas_call x1, Pallas kernels: 21.7 us -> 21.1 us  [shards(): pl.pallas_call(functools.partial(exchange_kernel, (dims, span, levels, ch...]
where the time goes in v4:
time: 23.1 us; the launch traced here: 22.8 us
  Pallas kernels  22.2 us (96%)
  between operations  0.64 us (3%)
    pallas_call x1, Pallas kernels, shards(): pl.pallas_call(functools.partial(exchange_kernel, (dims, span, levels, ch...  21.1 us
    pallas_call x1, Pallas kernels, shards(): pl.pallas_call(functools.partial(place_kernel, (dims, span, levels, field...  1.04 us

profile of v4, /device:TPU:13, one launch (start us, length us, event | category | flops | bytes accessed | tf_op | source)
XLA Modules:
  0.0 22.8 jit_solution(14648478189183952100)
XLA Ops:
  0.6 21.1 %exchange.1 = (f32[32,40,128]{2,1,0:T(8,128)S(1)}, s32[1,128]{1,0:T(1,128)S(4)}) custom-call(s32[16,128]{1,0:T(8,128)} %bitcast.4, s32[1,512]{1,0:T(1,128)} %keys_hbm.1, f32[2048,256]{1,0:T(8,128)} %measures_ref.1), custom_call_target="tpu_custom_call" | custom-call | tf_op jit(solution)/shard_map/exchange/pallas_call | solution.py:395
  21.8 1.0 %place.1 = (f32[512,256]{1,0:T(8,128)}, s32[1,512]{1,0:T(1,128)}, s32[1,512]{1,0:T(1,128)}, s32[1,1]{1,0:T(1,128)}) custom-call(s32[1,128]{1,0:T(1,128)S(4)} %get-tuple-element.10.counts_ref, f32[32,40,128]{2,1,0:T(8,128)S(1)} %get-tuple-element.11.recv_ref), custom_call_target="tpu_custom_call" | custom-call | tf_op jit(solution)/shard_map/place/pallas_call | solution.py:425

commit v5 on v4

--- a/solution.py
+++ b/solution.py
@@ -211,6 +211,7 @@
     row = lax.broadcasted_iota(jnp.int32, (span, LANES), 0)
     labels = lax.rem(row, levels) * devices + row // levels
 
+    pl.when(leads)(tell_leads)
     for c in range(chunks):
         loads[c].wait()
         x = held[pl.ds(c * chunk, chunk), :]
@@ -234,9 +235,10 @@
                 stage[:, h * levels : (h + 1) * levels, :] = block
             else:
                 stage[:, h * levels : (h + 1) * levels, :] += block
-        if c == 0:
+        if c == -1:
             pl.when(leads)(tell_leads)
-    pl.when(leads)(tell_above)
+        if c == 2:
+            pl.when(leads)(tell_above)
 
     tallies = lax.dot_general(
         jnp.ones((8, LANES), jnp.bfloat16),

time: 23.1 us -> 22.7 us (0.983)
  Pallas kernels: 22.2 us -> 21.8 us
    pallas_call x1, Pallas kernels: 21.1 us -> 20.7 us  [shards(): pl.pallas_call(functools.partial(exchange_kernel, (dims, span, levels, ch...]
where the time goes in v5:
time: 22.7 us; the launch traced here: 22.4 us
  Pallas kernels  21.8 us (96%)
  between operations  0.64 us (3%)
    pallas_call x1, Pallas kernels, shards(): pl.pallas_call(functools.partial(exchange_kernel, (dims, span, levels, ch...  20.7 us
    pallas_call x1, Pallas kernels, shards(): pl.pallas_call(functools.partial(place_kernel, (dims, span, levels, field...  1.04 us

profile of v5, /device:TPU:13, one launch (start us, length us, event | category | flops | bytes accessed | tf_op | source)
XLA Modules:
  0.0 22.4 jit_solution(1722462549780441892)
XLA Ops:
  0.6 20.7 %exchange.1 = (f32[32,40,128]{2,1,0:T(8,128)S(1)}, s32[1,128]{1,0:T(1,128)S(4)}) custom-call(s32[16,128]{1,0:T(8,128)} %bitcast.4, s32[1,512]{1,0:T(1,128)} %keys_hbm.1, f32[2048,256]{1,0:T(8,128)} %measures_ref.1), custom_call_target="tpu_custom_call" | custom-call | tf_op jit(solution)/shard_map/exchange/pallas_call | solution.py:397
  21.4 1.0 %place.1 = (f32[512,256]{1,0:T(8,128)}, s32[1,512]{1,0:T(1,128)}, s32[1,512]{1,0:T(1,128)}, s32[1,1]{1,0:T(1,128)}) custom-call(s32[1,128]{1,0:T(1,128)S(4)} %get-tuple-element.10.counts_ref, f32[32,40,128]{2,1,0:T(8,128)S(1)} %get-tuple-element.11.recv_ref), custom_call_target="tpu_custom_call" | custom-call | tf_op jit(solution)/shard_map/place/pallas_call | solution.py:427

commit v6 on v5

--- a/solution.py
+++ b/solution.py
@@ -46,7 +46,7 @@
         base = wrapped(side + s, sides) * half
         for c in range(half):
             for a in range(nx):
-                for b in range(ny):
+                for b in reversed(range(ny)):
                     targets.append(((jnp.int32(a), jnp.int32(b), base + c), s == sides))
     return targets
 
@@ -277,30 +277,35 @@
     shown = cbuf[...][:, 0, :]
     place = lax.broadcasted_iota(jnp.int32, shown.shape, 0)
     counts = jnp.sum(jnp.where(place == wide_chip, shown, 0), axis=0, keepdims=True)
-    before = jnp.sum(jnp.where(lane < me, counts, 0))
+    start_of = (modulo(place, plane) * cores + wide_core) * nz + divide(place, plane)
+    ahead = jnp.sum(jnp.where(start_of < me, shown, 0), axis=0, keepdims=True)
+    before = ahead[0, 0] + ahead[0, nz] if cores == 2 else ahead[0, 0]
     shift = modulo(before, devices)
 
     targets = targets_of(spots, dims)
     piece = pl.ds(0, sent_rows)
-    for across in (False, True) if any(not own for _, own in targets) else (True,):
-        for spot, own in targets:
-            if own == across:
-                other = flat(spot, dims)
-                send[other] = stage[modulo(other - shift + devices, devices)]
-        for spot, own in targets:
-            if own == across:
-                other = flat(spot, dims)
-                copy = remote(
-                    send.at[other, piece],
-                    recv_ref.at[me, piece],
-                    data_sem.at[0],
-                    data_sem.at[1],
-                    spot,
-                )
-                if own:
-                    pl.when(other != me)(copy.start)
-                else:
-                    copy.start()
+    far = [target for target in targets if not target[1]]
+    near = [target for target in targets if target[1]]
+    mixed = far[: len(far) // 2]
+    for k, target in enumerate(far[len(far) // 2 :]):
+        mixed += [target] + near[2 * k : 2 * k + 2]
+    mixed += near[2 * (len(far) - len(far) // 2) :]
+    for spot, _ in mixed:
+        other = flat(spot, dims)
+        send[other] = stage[modulo(other - shift + devices, devices)]
+    for spot, own in mixed:
+        other = flat(spot, dims)
+        copy = remote(
+            send.at[other, piece],
+            recv_ref.at[me, piece],
+            data_sem.at[0],
+            data_sem.at[1],
+            spot,
+        )
+        if own:
+            pl.when(other != me)(copy.start)
+        else:
+            copy.start()
     recv_ref[me] = send[me]
     counts_kept[...] = counts
     counts_copy = pltpu.make_async_copy(counts_kept, counts_ref, small_sem.at[4])
@@ -343,14 +348,13 @@
     starts, turns = [], []
     for d in range(devices):
         first = modulo(me - modulo(offset, devices) + devices, devices)
-        start = divide(offset + first, devices)
-        for h in range(halves):
-            buf[h, pl.ds(start, levels), :] = recv_ref[d, h * levels : (h + 1) * levels, :]
-        starts.append(start)
-        turns.append(modulo(start - first * levels + span, LANES))
+        starts.append(divide(offset + first, devices))
+        turns.append(modulo(starts[d] - first * levels + span, LANES))
         offset = offset + counts_ref[0, d]
     copies = []
     for h in range(halves):
+        for d in range(devices):
+            buf[h, pl.ds(starts[d], levels), :] = recv_ref[d, h * levels : (h + 1) * levels, :]
         copies.append(
             pltpu.make_async_copy(
                 buf.at[h, pl.ds(0, span)], sums_ref.at[:, pl.ds(h * LANES, LANES)], sems.at[h]

time: 22.7 us -> 22.6 us (level)
  the two profiles are of different devices: /device:TPU:13 before, /device:TPU:12 now
where the time goes in v6:
time: 22.6 us; the launch traced here: 22.4 us
  Pallas kernels  21.8 us (96%)
  between operations  0.64 us (3%)
    pallas_call x1, Pallas kernels, shards(): pl.pallas_call(functools.partial(exchange_kernel, (dims, span, levels, ch...  20.8 us
    pallas_call x1, Pallas kernels, shards(): pl.pallas_call(functools.partial(place_kernel, (dims, span, levels, field...  1.01 us

profile of v6, /device:TPU:12, one launch (start us, length us, event | category | flops | bytes accessed | tf_op | source)
XLA Modules:
  0.0 22.4 jit_solution(7876067163879182731)
XLA Ops:
  0.6 20.8 %exchange.1 = (f32[32,40,128]{2,1,0:T(8,128)S(1)}, s32[1,128]{1,0:T(1,128)S(4)}) custom-call(s32[16,128]{1,0:T(8,128)} %bitcast.4, s32[1,512]{1,0:T(1,128)} %keys_hbm.1, f32[2048,256]{1,0:T(8,128)} %measures_ref.1), custom_call_target="tpu_custom_call" | custom-call | tf_op jit(solution)/shard_map/exchange/pallas_call | solution.py:401
  21.4 1.0 %place.1 = (f32[512,256]{1,0:T(8,128)}, s32[1,512]{1,0:T(1,128)}, s32[1,512]{1,0:T(1,128)}, s32[1,1]{1,0:T(1,128)}) custom-call(s32[1,128]{1,0:T(1,128)S(4)} %get-tuple-element.10.counts_ref, f32[32,40,128]{2,1,0:T(8,128)S(1)} %get-tuple-element.11.recv_ref), custom_call_target="tpu_custom_call" | custom-call | tf_op jit(solution)/shard_map/place/pallas_call | solution.py:431

commit v7 on v6

--- a/solution.py
+++ b/solution.py
@@ -237,7 +237,7 @@
                 stage[:, h * levels : (h + 1) * levels, :] += block
         if c == -1:
             pl.when(leads)(tell_leads)
-        if c == 2:
+        if c == min(2, chunks - 1):
             pl.when(leads)(tell_above)
 
     tallies = lax.dot_general(

time: 22.6 us -> 22.6 us (level)
  no operation moved by 1% of the time
where the time goes in v7:
time: 22.6 us; the launch traced here: 22.4 us
  Pallas kernels  21.8 us (96%)
  between operations  0.64 us (3%)
    pallas_call x1, Pallas kernels, shards(): pl.pallas_call(functools.partial(exchange_kernel, (dims, span, levels, ch...  20.8 us
    pallas_call x1, Pallas kernels, shards(): pl.pallas_call(functools.partial(place_kernel, (dims, span, levels, field...  1.01 us

profile of v7, /device:TPU:12, one launch (start us, length us, event | category | flops | bytes accessed | tf_op | source)
XLA Modules:
  0.0 22.4 jit_solution(7876067163879182731)
XLA Ops:
  0.6 20.8 %exchange.1 = (f32[32,40,128]{2,1,0:T(8,128)S(1)}, s32[1,128]{1,0:T(1,128)S(4)}) custom-call(s32[16,128]{1,0:T(8,128)} %bitcast.4, s32[1,512]{1,0:T(1,128)} %keys_hbm.1, f32[2048,256]{1,0:T(8,128)} %measures_ref.1), custom_call_target="tpu_custom_call" | custom-call | tf_op jit(solution)/shard_map/exchange/pallas_call | solution.py:401
  21.4 1.0 %place.1 = (f32[512,256]{1,0:T(8,128)}, s32[1,512]{1,0:T(1,128)}, s32[1,512]{1,0:T(1,128)}, s32[1,1]{1,0:T(1,128)}) custom-call(s32[1,128]{1,0:T(1,128)S(4)} %get-tuple-element.10.counts_ref, f32[32,40,128]{2,1,0:T(8,128)S(1)} %get-tuple-element.11.recv_ref), custom_call_target="tpu_custom_call" | custom-call | tf_op jit(solution)/shard_map/place/pallas_call | solution.py:431
